TPU v7x, 32 devices: a whole 2x2x4 slice. The times are simulated.
32 devices in a mesh: clip: 16 (over z, y, x), mp: 2 (over core).
Axes of the slice: x: 2, y: 2, z: 4, core: 2. Of those that a mesh axis runs over, the one named last changes fastest.
Arguments:
- tokens: bfloat16 [48, 128, 1024], P('clip', None, 'mp'), may hold values from -6 to 6
- bottleneck: bfloat16 [16, 4, 1024], P('clip', None, 'mp'), may hold values from -6 to 6
- clip_lengths: int32 [16], replicated, may hold values from 2 to 4, as said below
- video_blocks: int32 [16], replicated, may hold values from 1 to 3, as said below
- store_map: int32 [16, 3], replicated, may hold values from -1 to 63, as said below
- norm1_gain: float32 [1024], replicated, may hold values from 0.4 to 1.6
- w_qkv: bfloat16 [3, 1024, 1024], P(None, None, 'mp'), may hold values from -0.625 to 0.625
- w_out: bfloat16 [1024, 1024], P('mp'), may hold values from -0.1875 to 0.1875
- norm2_gain: float32 [1024], replicated, may hold values from 0.4 to 1.6
- w_up: bfloat16 [1024, 4096], P(None, 'mp'), may hold values from -0.1875 to 0.1875
- w_down: bfloat16 [4096, 1024], P('mp'), may hold values from -0.09375 to 0.09375
Outputs:
- mixed_tokens: bfloat16 [48, 128, 1024], P('clip', None, 'mp')
- merged_bottleneck: bfloat16 [16, 4, 1024], P('clip', None, 'mp')
Inputs may be any that keep to these rules, and one draw needn't show every extreme that they name: clip_lengths[c] counts the blocks of the clip owned by index c of clip. The first video_blocks[c] blocks of clip c are video, the others up to clip_lengths[c] audio; video_blocks[c] <= clip_lengths[c] - 1. store_map[d, s] = c * 4 + b when slot s of device d along clip holds block b of clip c, and -1 when the slot is empty; each block b < clip_lengths[c] of each clip sits in exactly one slot, on a device of the same aligned group of 4 devices along clip as c; no device holds two blocks of one clip.
All inputs are finite; a program needn't handle non-finite values.
Results may differ from a plain program's by a relative error of at most 0.006.
Values may be sent and summed in bfloat16 or wider, within the bound.
A program may use at most 128 MiB of HBM per device.

v0:
```python
import jax
import jax.numpy as jnp
from jax import lax
from jax.sharding import PartitionSpec as P

HEAD_DIM = 64
BLK = 128
NB = 4
SLOT_DEV = 4
STORE_DEV = 3
GROUP = 4


def partner(x, axis, stride):
    return lax.ppermute(x, axis, [(i, i ^ 1 << stride) for i in range(lax.axis_size(axis))])


def layer_norm(rows, gain):
    mean = jnp.mean(rows, axis=-1, keepdims=True)
    centred = rows - mean
    moment = jnp.mean(centred * centred, axis=-1, keepdims=True)
    return centred * lax.rsqrt(moment + 1e-05) * gain


def attend(scores, allowed, values):
    masked = jnp.where(allowed, scores, -1e30)
    top = jnp.max(masked, axis=-1, keepdims=True)
    weights = jnp.where(allowed, jnp.exp(masked - top), 0.0)
    weights = (weights / jnp.sum(weights, axis=-1, keepdims=True)).astype(jnp.bfloat16)
    return jnp.dot(weights, values, preferred_element_type=jnp.float32)


def owner_sections(buffer):
    width = buffer.shape[2]
    for bit in range(GROUP.bit_length() - 1):
        stride = 1 << bit
        shaped = buffer.reshape(GROUP // (2 * stride), 2, stride, BLK, width)
        arrived = partner(shaped[:, 1], "clip", bit)
        buffer = jnp.stack([shaped[:, 0], arrived], axis=1).reshape(GROUP, BLK, width)
    return buffer


def store_sections(buffer):
    width = buffer.shape[2]
    for bit in range(GROUP.bit_length() - 1):
        stride = 1 << bit
        shaped = buffer.reshape(GROUP // (2 * stride), 2, stride, BLK, width)
        arrived = partner(shaped[:, 1], "clip", bit)
        buffer = jnp.stack([shaped[:, 0], arrived], axis=1).reshape(GROUP, BLK, width)
    return buffer


def body(
    tokens,
    bottleneck,
    clip_lengths,
    video_blocks,
    store_map,
    norm1_gain,
    w_qkv,
    w_out,
    norm2_gain,
    w_up,
    w_down,
):
    member = lax.axis_index("clip")
    width = tokens.shape[2]
    total_rows = SLOT_DEV * BLK
    own_map = lax.dynamic_index_in_dim(store_map, member, 0, keepdims=False)
    owner_of = jnp.where(own_map >= 0, own_map // SLOT_DEV, -1)
    wanted = member * SLOT_DEV + jnp.arange(SLOT_DEV, dtype=jnp.int32)
    partners = jnp.bitwise_xor(member, jnp.arange(GROUP, dtype=jnp.int32))
    pick_near = (owner_of[None, :] == partners[:, None]).astype(jnp.bfloat16)
    partner_maps = jnp.take(store_map, partners, axis=0)
    came_near = jnp.any(partner_maps[None, :, :] == wanted[:, None, None], axis=2).astype(
        jnp.bfloat16
    )
    outgoing = jnp.einsum(
        "rs,sxd->rxd", pick_near, tokens, preferred_element_type=jnp.float32
    ).astype(jnp.bfloat16)
    arrived = owner_sections(outgoing)
    clip_blocks = jnp.einsum(
        "br,rxd->bxd", came_near, arrived, preferred_element_type=jnp.float32
    ).astype(jnp.bfloat16)
    rows = jnp.concatenate([clip_blocks.reshape(total_rows, width), bottleneck[0]], axis=0)
    whole = lax.all_gather(rows, "mp", axis=1, tiled=True)
    normed = layer_norm(whole.astype(jnp.float32), norm1_gain).astype(jnp.bfloat16)
    query = jnp.dot(normed, w_qkv[0], preferred_element_type=jnp.float32).astype(jnp.bfloat16)
    keys = jnp.dot(normed, w_qkv[1], preferred_element_type=jnp.float32).astype(jnp.bfloat16)
    values = jnp.dot(normed, w_qkv[2], preferred_element_type=jnp.float32).astype(jnp.bfloat16)
    length = lax.dynamic_index_in_dim(clip_lengths, member, 0, keepdims=False)
    video = lax.dynamic_index_in_dim(video_blocks, member, 0, keepdims=False)
    block_of = jnp.arange(total_rows, dtype=jnp.int32) // BLK
    token_mode = jnp.where(block_of < video, 0, jnp.where(block_of < length, 1, -1)).astype(
        jnp.int32
    )
    key_mode = jnp.concatenate([token_mode, jnp.full((NB,), 2, jnp.int32)])
    token_allow = (key_mode[None, :] == token_mode[:, None]) | (key_mode[None, :] == 2)
    video_allow = jnp.broadcast_to((key_mode == 0) | (key_mode == 2), (NB, total_rows + NB))
    audio_allow = jnp.broadcast_to((key_mode == 1) | (key_mode == 2), (NB, total_rows + NB))
    local_heads = w_qkv.shape[2] // HEAD_DIM
    pieces = []
    for head in range(local_heads):
        cols = slice(head * HEAD_DIM, (head + 1) * HEAD_DIM)
        scores = lax.dot_general(
            query[:, cols],
            keys[:, cols],
            (((1,), (1,)), ((), ())),
            preferred_element_type=jnp.float32,
        )
        scores = scores * HEAD_DIM ** (-0.5)
        own = attend(scores[:total_rows], token_allow, values[:, cols])
        seen_video = attend(scores[total_rows:], video_allow, values[:, cols])
        seen_audio = attend(scores[total_rows:], audio_allow, values[:, cols])
        pieces.append(jnp.concatenate([own, 0.5 * (seen_video + seen_audio)], axis=0))
    context = jnp.concatenate(pieces, axis=1).astype(jnp.bfloat16)
    projected = jnp.dot(context, w_out, preferred_element_type=jnp.float32)
    attended = lax.psum_scatter(projected, "mp", scatter_dimension=1, tiled=True)
    after = (rows.astype(jnp.float32) + attended).astype(jnp.bfloat16)
    outgoing = jnp.einsum(
        "br,bxd->rxd",
        came_near,
        after[:total_rows].reshape(SLOT_DEV, BLK, width),
        preferred_element_type=jnp.float32,
    ).astype(jnp.bfloat16)
    arrived = store_sections(outgoing)
    returned = jnp.einsum(
        "rs,rxd->sxd", pick_near, arrived, preferred_element_type=jnp.float32
    ).astype(jnp.bfloat16)
    joined = jnp.concatenate([returned.reshape(STORE_DEV * BLK, width), after[total_rows:]], axis=0)
    whole = lax.all_gather(joined, "mp", axis=1, tiled=True)
    normed = layer_norm(whole.astype(jnp.float32), norm2_gain).astype(jnp.bfloat16)
    active = jax.nn.gelu(
        jnp.dot(normed, w_up, preferred_element_type=jnp.float32), approximate=True
    ).astype(jnp.bfloat16)
    partial_sum = jnp.dot(active, w_down, preferred_element_type=jnp.float32)
    added = lax.psum_scatter(partial_sum, "mp", scatter_dimension=1, tiled=True)
    merged = (joined.astype(jnp.float32) + added).astype(jnp.bfloat16)
    stored = merged[: STORE_DEV * BLK].reshape(STORE_DEV, BLK, width)
    merged_extra = merged[STORE_DEV * BLK :]
    mixed_tokens = jnp.where(own_map[:, None, None] >= 0, stored, jnp.zeros_like(stored))
    return (mixed_tokens, merged_extra[None])


def solution(mesh):
    placed = (
        P("clip", None, "mp"),
        P("clip", None, "mp"),
        P(),
        P(),
        P(),
        P(),
        P(None, None, "mp"),
        P("mp", None),
        P(),
        P(None, "mp"),
        P("mp", None),
    )
    return jax.shard_map(
        body,
        mesh=mesh,
        in_specs=placed,
        out_specs=(P("clip", None, "mp"), P("clip", None, "mp")),
        check_vma=False,
    )
```

profile of v0, /device:TPU:0, one launch (start us, length us, event | category | flops | bytes accessed | tf_op | source)
XLA Modules:
  0.0 156.6 jit_solution(16660955386779885300)
XLA Ops:
  11.7 3.0 %collective-permute-start = (bf16[2,1,128,512]{3,2,0,1:T(8,128)(2,1)S(1)}, bf16[2,1,128,512]{3,2,0,1:T(8,128)(2,1)S(1)}, u32[]{:S(2)}, u32[]{:S(2)}) collective-permute-start(bf16[2,1,128,512]{3,2,0,1:T(8,128)(2,1)S(1)} %bitcast.70), channel_id=1, source_target_pairs={{0,2},{2,0},{4,6},{6,4},{8,10},{10,8},{12,14},{14,12},{16,18},{18,... | collective-permute-start | bytes 786440 | tf_op jit(solution)/shard_map/ppermute | solution.py:15
  15.5 5.5 %collective-permute-done = bf16[2,1,128,512]{3,2,0,1:T(8,128)(2,1)S(1)} collective-permute-done((bf16[2,1,128,512]{3,2,0,1:T(8,128)(2,1)S(1)}, bf16[2,1,128,512]{3,2,0,1:T(8,128)(2,1)S(1)}, u32[]{:S(2)}, u32[]{:S(2)}) %collective-permute-start) | collective-permute-done | bytes 262176 | tf_op jit(solution)/shard_map/ppermute | solution.py:15
  21.2 1.8 %collective-permute-start.1 = (bf16[1,2,128,512]{3,2,1,0:T(8,128)(2,1)S(1)}, bf16[1,2,128,512]{3,2,1,0:T(8,128)(2,1)S(1)}, u32[]{:S(2)}, u32[]{:S(2)}) collective-permute-start(bf16[1,2,128,512]{3,2,1,0:T(8,128)(2,1)S(1)} %get-tuple-element.80), channel_id=1, source_target_pairs={{0,4},{2,6},{4,0},{6,2},{8,12},{10,14},{12,8},{14,10},{16,20},{18,... | collective-permute-start | bytes 786440 | tf_op jit(solution)/shard_map/ppermute | solution.py:15
  23.3 5.4 %collective-permute-done.1 = bf16[1,2,128,512]{3,2,1,0:T(8,128)(2,1)S(1)} collective-permute-done((bf16[1,2,128,512]{3,2,1,0:T(8,128)(2,1)S(1)}, bf16[1,2,128,512]{3,2,1,0:T(8,128)(2,1)S(1)}, u32[]{:S(2)}, u32[]{:S(2)}) %collective-permute-start.1) | collective-permute-done | bytes 262176 | tf_op jit(solution)/shard_map/ppermute | solution.py:15
  33.8 7.7 %all-gather.2.cloned.1.call-done = bf16[516,1024]{1,0:T(8,128)(2,1)} async-done(((bf16[516,512]{1,0:T(8,128)(2,1)}), bf16[516,1024]{1,0:T(8,128)(2,1)}) %all-gather.2.cloned.1.call-update) | async-done | bytes 1056784 | tf_op jit(solution)/shard_map/all_gather | solution.py:86
  43.6 2.3 %convolution_convert_fusion.1 = bf16[516,512]{1,0:T(8,128)(2,1)S(1)} fusion(bf16[3,1024,512]{2,1,0:T(8,128)(2,1)} %param.17, bf16[516,1024]{1,0:T(8,128)(2,1)S(1)} %copy-done.15, f32[1024]{0:T(1024)S(1)} %copy-done.19, f32[516]{0:T(1024)S(1)} %add_rsqrt_fusion, f32[516]{0:T(1024)S(1)} %broadcast_multiply_fusion), kind=kOutput, calls=%fused_computation.63 | convolution fusion | flops 543971328 | bytes 2641952 | tf_op jit(solution)/shard_map/dot_general | solution.py:89
  53.4 5.2 %fusion.53 = (f32[512]{0:T(512)S(1)}, f32[512]{0:T(512)S(1)}, f32[512]{0:T(512)S(1)}, f32[512]{0:T(512)S(1)}, f32[512]{0:T(512)S(1)}, /*index=5*/f32[512]{0:T(512)S(1)}, f32[512]{0:T(512)S(1)}) fusion(f32[516,516]{1,0:T(8,128)S(1)} %convolution_multiply_fusion, s32[516]{0:T(1024)S(1)} %concatenate.46, s32[512]{0:T(512)S(1)} %select_select_fusion, ...), kind=kLoop, calls=%fused_computation.115 | loop fusion | flops 4223488 | bytes 7416340 | tf_op jit(solution)/shard_map/reduce_max | solution.py:27
  59.0 4.5 %fusion.195 = (f32[512]{0:T(512)S(1)}, f32[512]{0:T(512)S(1)}, f32[512]{0:T(512)S(1)}, f32[512]{0:T(512)S(1)}, f32[512]{0:T(512)S(1)}, /*index=5*/f32[512]{0:T(512)S(1)}, f32[512]{0:T(512)S(1)}, f32[512]{0:T(512)S(1)}) fusion(f32[512]{0:T(512)S(1)} %get-tuple-element.42, f32[516,516]{1,0:T(8,128)S(1)} %convolution_multiply_fusion, ...), kind=kLoop, calls=%fused_computation.344 | loop fusion | flops 8450048 | bytes 8489492 | tf_op jit(solution)/shard_map/reduce_sum | solution.py:29
  65.8 2.2 %convolution_convert_fusion.13 = bf16[512,64]{0,1:T(8,128)(2,1)S(1)} fusion(f32[512]{0:T(512)S(1)} %get-tuple-element.40, bf16[516,512]{1,0:T(8,128)(2,1)} %copy-done.23, f32[516,516]{1,0:T(8,128)} %copy-done.11, f32[512]{0:T(512)S(1)} %get-tuple-element.48, s32[516]{0:T(1024)S(1)} %concatenate.46, s32[512]{0:T(512)S(1)} %select_select_fusion, ...), kind=kOutput, calls=%fused_computation.75 | convolution fusion | flops 35698688 | bytes 1518100 | tf_op jit(solution)/shard_map/dot_general | solution.py:30
  70.0 2.1 %convolution_convert_fusion.12 = bf16[512,64]{0,1:T(8,128)(2,1)S(1)} fusion(f32[512]{0:T(512)S(1)} %get-tuple-element.39, bf16[516,512]{1,0:T(8,128)(2,1)} %copy-done.23, f32[516,516]{1,0:T(8,128)} %copy-done.9, f32[512]{0:T(512)S(1)} %get-tuple-element.47, s32[516]{0:T(1024)S(1)} %concatenate.46, s32[512]{0:T(512)S(1)} %select_select_fusion, ...), kind=kOutput, calls=%fused_computation.74 | convolution fusion | flops 35698688 | bytes 1518100 | tf_op jit(solution)/shard_map/dot_general | solution.py:30
  74.2 2.2 %convolution_convert_fusion.11 = bf16[512,64]{0,1:T(8,128)(2,1)S(1)} fusion(f32[512]{0:T(512)S(1)} %get-tuple-element.38, bf16[516,512]{1,0:T(8,128)(2,1)} %copy-done.23, f32[516,516]{1,0:T(8,128)} %copy-done.7, f32[512]{0:T(512)S(1)} %get-tuple-element.46, s32[516]{0:T(1024)S(1)} %concatenate.46, s32[512]{0:T(512)S(1)} %select_select_fusion, ...), kind=kOutput, calls=%fused_computation.73 | convolution fusion | flops 35698688 | bytes 1518100 | tf_op jit(solution)/shard_map/dot_general | solution.py:30
  78.4 2.1 %convolution_convert_fusion.10 = bf16[512,64]{0,1:T(8,128)(2,1)S(1)} fusion(f32[512]{0:T(512)S(1)} %get-tuple-element.37, bf16[516,512]{1,0:T(8,128)(2,1)} %copy-done.23, f32[516,516]{1,0:T(8,128)} %copy-done.5, f32[512]{0:T(512)S(1)} %get-tuple-element.45, s32[516]{0:T(1024)S(1)} %concatenate.46, s32[512]{0:T(512)S(1)} %select_select_fusion, ...), kind=kOutput, calls=%fused_computation.72 | convolution fusion | flops 35698688 | bytes 1518100 | tf_op jit(solution)/shard_map/dot_general | solution.py:30
  82.6 2.2 %convolution_convert_fusion.9 = bf16[512,64]{0,1:T(8,128)(2,1)S(1)} fusion(f32[512]{0:T(512)S(1)} %get-tuple-element.36, bf16[516,512]{1,0:T(8,128)(2,1)} %copy-done.23, f32[516,516]{1,0:T(8,128)} %copy-done.3, f32[512]{0:T(512)S(1)} %get-tuple-element.44, s32[516]{0:T(1024)S(1)} %concatenate.46, s32[512]{0:T(512)S(1)} %select_select_fusion, ...), kind=kOutput, calls=%fused_computation.71 | convolution fusion | flops 35698688 | bytes 1518100 | tf_op jit(solution)/shard_map/dot_general | solution.py:30
  86.8 2.1 %convolution_convert_fusion.8 = bf16[512,64]{0,1:T(8,128)(2,1)S(1)} fusion(f32[512]{0:T(512)S(1)} %get-tuple-element.35, bf16[516,512]{1,0:T(8,128)(2,1)} %copy-done.23, f32[516,516]{1,0:T(8,128)} %copy-done.1, f32[512]{0:T(512)S(1)} %get-tuple-element.43, s32[516]{0:T(1024)S(1)} %concatenate.46, s32[512]{0:T(512)S(1)} %select_select_fusion, ...), kind=kOutput, calls=%fused_computation.70 | convolution fusion | flops 35698688 | bytes 1518100 | tf_op jit(solution)/shard_map/dot_general | solution.py:30
  89.5 1.7 %convolution_convert_fusion.7 = bf16[512,64]{0,1:T(8,128)(2,1)S(1)} fusion(f32[512]{0:T(512)S(1)} %get-tuple-element.34, bf16[516,512]{1,0:T(8,128)(2,1)} %copy-done.23, f32[516,516]{1,0:T(8,128)S(1)} %convolution_multiply_fusion, f32[512]{0:T(512)S(1)} %get-tuple-element.42, s32[516]{0:T(1024)S(1)} %concatenate.46, s32[512]{0:T(512)S(1)} %select_select_fusion, ...), kind=kOutput, calls=%fused_computation.69 | convolution fusion | flops 35698688 | bytes 1520640 | tf_op jit(solution)/shard_map/dot_general | solution.py:30
  91.4 2.1 %fusion.204 = f32[516,1024]{1,0:T(8,128)} fusion(bf16[516,512]{0,1:T(8,128)(2,1)S(1)} %maximum_dynamic-update-slice_fusion, bf16[512,1024]{1,0:T(8,128)(2,1)S(1)} %copy-done), kind=kOutput, calls=%fused_computation.350 | convolution fusion | flops 541065216 | bytes 3690496 | tf_op jit(solution)/shard_map/dot_general | solution.py:117
  93.9 10.7 %reduce-scatter.3.cloned.1.call-done = f32[516,512]{1,0:T(8,128)} async-done(((f32[516,1024]{1,0:T(8,128)}), f32[516,512]{1,0:T(8,128)}) %reduce-scatter.3.cloned.1.call-update) | async-done | bytes 1056784 | tf_op jit(solution)/shard_map/reduce_scatter | solution.py:118
  107.7 1.9 %collective-permute-start.2 = (bf16[2,1,128,512]{3,2,0,1:T(8,128)(2,1)S(1)}, bf16[2,1,128,512]{3,2,0,1:T(8,128)(2,1)S(1)}, u32[]{:S(2)}, u32[]{:S(2)}) collective-permute-start(bf16[2,1,128,512]{3,2,0,1:T(8,128)(2,1)S(1)} %bitcast.71), channel_id=1, source_target_pairs={{0,2},{2,0},{4,6},{6,4},{8,10},{10,8},{12,14},{14,12},{16,18},{18,... | collective-permute-start | bytes 786440 | tf_op jit(solution)/shard_map/ppermute | solution.py:15
  109.6 6.6 %collective-permute-done.2 = bf16[2,1,128,512]{3,2,0,1:T(8,128)(2,1)S(1)} collective-permute-done((bf16[2,1,128,512]{3,2,0,1:T(8,128)(2,1)S(1)}, bf16[2,1,128,512]{3,2,0,1:T(8,128)(2,1)S(1)}, u32[]{:S(2)}, u32[]{:S(2)}) %collective-permute-start.2) | collective-permute-done | bytes 262176 | tf_op jit(solution)/shard_map/ppermute | solution.py:15
  116.4 1.7 %collective-permute-start.3 = (bf16[1,2,128,512]{3,2,1,0:T(8,128)(2,1)S(1)}, bf16[1,2,128,512]{3,2,1,0:T(8,128)(2,1)S(1)}, u32[]{:S(2)}, u32[]{:S(2)}) collective-permute-start(bf16[1,2,128,512]{3,2,1,0:T(8,128)(2,1)S(1)} %get-tuple-element.76), channel_id=1, source_target_pairs={{0,4},{2,6},{4,0},{6,2},{8,12},{10,14},{12,8},{14,10},{16,20},{18,... | collective-permute-start | bytes 786440 | tf_op jit(solution)/shard_map/ppermute | solution.py:15
  118.1 6.0 %collective-permute-done.3 = bf16[1,2,128,512]{3,2,1,0:T(8,128)(2,1)S(1)} collective-permute-done((bf16[1,2,128,512]{3,2,1,0:T(8,128)(2,1)S(1)}, bf16[1,2,128,512]{3,2,1,0:T(8,128)(2,1)S(1)}, u32[]{:S(2)}, u32[]{:S(2)}) %collective-permute-start.3) | collective-permute-done | bytes 262176 | tf_op jit(solution)/shard_map/ppermute | solution.py:15
  125.6 2.4 %all_gather.7 = bf16[388,1024]{1,0:T(8,128)(2,1)S(1)} all-gather(bf16[388,512]{1,0:T(8,128)(2,1)S(1)} %pad_maximum_fusion.3), channel_id=1, replica_groups=mesh['clip'=16,'mp'=2] {'mp'}, dimensions={1}, use_global_device_ids=true | all-gather | bytes 1191936 | tf_op jit(solution)/shard_map/all_gather | solution.py:131
  128.5 8.7 %fusion.18 = f32[388,1024]{1,0:T(8,128)} fusion(bf16[2048,1024]{1,0:T(8,128)(2,1)} %param.21, bf16[1024,2048]{1,0:T(8,128)(2,1)} %param.20, bf16[388,1024]{1,0:T(8,128)(2,1)S(1)} %all_gather.7, f32[1024]{0:T(1024)S(1)} %copy-done.20, f32[388]{0:T(512)S(1)} %add_rsqrt_fusion.1, f32[388]{0:T(512)S(1)} %broadcast_multiply_fusion.1), kind=kOutput, calls=%fused_computation.24 | convolution fusion | flops 3263918080 | bytes 10779680 | tf_op jit(solution)/shard_map/dot_general | solution.py:136
  137.2 10.1 %reduce-scatter.5.cloned.1.call-done = f32[388,512]{1,0:T(8,128)} async-done(((f32[388,1024]{1,0:T(8,128)}), f32[388,512]{1,0:T(8,128)}) %reduce-scatter.5.cloned.1.call-update) | async-done | bytes 794640 | tf_op jit(solution)/shard_map/reduce_scatter | solution.py:137
  (173 shorter events, 41.5 us)
Async XLA Ops:
  7.2 84.3 %copy-start = (bf16[512,1024]{1,0:T(8,128)(2,1)S(1)}, bf16[512,1024]{1,0:T(8,128)(2,1)}, u32[]{:S(2)}) copy-start(bf16[512,1024]{1,0:T(8,128)(2,1)} %param.18) | copy-start | bytes 3145732
  7.2 34.3 %all-gather.2.cloned.1.call-start = ((), (), s32[]{:S(2)}) async-start(), calls=%async_computation.2 | async-start | bytes 1597440 | tf_op jit(solution)/shard_map/all_gather | solution.py:86
  10.9 3.9 %copy-start.16 = (s32[16,3]{0,1:T(4,128)S(1)}, s32[16,3]{0,1:T(4,128)}, u32[]{:S(2)}) copy-start(s32[16,3]{0,1:T(4,128)} %param.15) | copy-start | bytes 580
  11.7 9.3 %collective-permute-start = (bf16[2,1,128,512]{3,2,0,1:T(8,128)(2,1)S(1)}, bf16[2,1,128,512]{3,2,0,1:T(8,128)(2,1)S(1)}, u32[]{:S(2)}, u32[]{:S(2)}) collective-permute-start(bf16[2,1,128,512]{3,2,0,1:T(8,128)(2,1)S(1)} %bitcast.70), channel_id=1, source_target_pairs={{0,2},{2,0},{4,6},{6,4},{8,10},{10,8},{12,14},{14,12},{16,18},{18,... | collective-permute-start | bytes 786440 | tf_op jit(solution)/shard_map/ppermute | solution.py:15
  21.2 7.5 %collective-permute-start.1 = (bf16[1,2,128,512]{3,2,1,0:T(8,128)(2,1)S(1)}, bf16[1,2,128,512]{3,2,1,0:T(8,128)(2,1)S(1)}, u32[]{:S(2)}, u32[]{:S(2)}) collective-permute-start(bf16[1,2,128,512]{3,2,1,0:T(8,128)(2,1)S(1)} %get-tuple-element.80), channel_id=1, source_target_pairs={{0,4},{2,6},{4,0},{6,2},{8,12},{10,14},{12,8},{14,10},{16,20},{18,... | collective-permute-start | bytes 786440 | tf_op jit(solution)/shard_map/ppermute | solution.py:15
  31.1 12.5 %copy-start.19 = (f32[1024]{0:T(1024)S(1)}, f32[1024]{0:T(1024)}, u32[]{:S(2)}) copy-start(f32[1024]{0:T(1024)} %param.16) | copy-start | bytes 12292
  31.1 73.4 %reduce-scatter.3.cloned.1.call-start = ((), (), s32[]{:S(2)}) async-start(), calls=%async_computation.3 | async-start | bytes 3194880 | tf_op jit(solution)/shard_map/reduce_scatter | solution.py:118
  43.5 2.3 %copy-start.18 = (bf16[3,1024,512]{2,1,0:T(8,128)(2,1)S(1)}, bf16[3,1024,512]{2,1,0:T(8,128)(2,1)}, u32[]{:S(2)}) copy-start(bf16[3,1024,512]{2,1,0:T(8,128)(2,1)} %param.17) | copy-start | bytes 9437188
  47.3 3.6 %copy-start.11 = (f32[516,516]{1,0:T(8,128)}, f32[516,516]{1,0:T(8,128)S(1)}, u32[]{:S(2)}) copy-start(f32[516,516]{1,0:T(8,128)S(1)} %convolution_multiply_fusion.6) | copy-start | bytes 3195076
  48.1 2.4 %copy-start.1 = (f32[516,516]{1,0:T(8,128)}, f32[516,516]{1,0:T(8,128)S(1)}, u32[]{:S(2)}) copy-start(f32[516,516]{1,0:T(8,128)S(1)} %convolution_multiply_fusion.1) | copy-start | bytes 3195076
  49.8 2.6 %copy-start.13 = (f32[516,516]{1,0:T(8,128)}, f32[516,516]{1,0:T(8,128)S(1)}, u32[]{:S(2)}) copy-start(f32[516,516]{1,0:T(8,128)S(1)} %convolution_multiply_fusion.7) | copy-start | bytes 3195076
  53.3 5.3 %copy-start.2 = (f32[516,516]{1,0:T(8,128)S(1)}, f32[516,516]{1,0:T(8,128)}, u32[]{:S(2)}) copy-start(f32[516,516]{1,0:T(8,128)} %copy-done.1) | copy-start | bytes 3195076
  53.3 5.3 %copy-start.4 = (f32[516,516]{1,0:T(8,128)S(1)}, f32[516,516]{1,0:T(8,128)}, u32[]{:S(2)}) copy-start(f32[516,516]{1,0:T(8,128)} %copy-done.3) | copy-start | bytes 3195076
  53.3 5.3 %copy-start.6 = (f32[516,516]{1,0:T(8,128)S(1)}, f32[516,516]{1,0:T(8,128)}, u32[]{:S(2)}) copy-start(f32[516,516]{1,0:T(8,128)} %copy-done.5) | copy-start | bytes 3195076
  53.3 5.3 %copy-start.8 = (f32[516,516]{1,0:T(8,128)S(1)}, f32[516,516]{1,0:T(8,128)}, u32[]{:S(2)}) copy-start(f32[516,516]{1,0:T(8,128)} %copy-done.7) | copy-start | bytes 3195076
  53.4 5.3 %copy-start.10 = (f32[516,516]{1,0:T(8,128)S(1)}, f32[516,516]{1,0:T(8,128)}, u32[]{:S(2)}) copy-start(f32[516,516]{1,0:T(8,128)} %copy-done.9) | copy-start | bytes 3195076
  53.4 5.6 %copy-start.12 = (f32[516,516]{1,0:T(8,128)S(1)}, f32[516,516]{1,0:T(8,128)}, u32[]{:S(2)}) copy-start(f32[516,516]{1,0:T(8,128)} %copy-done.11) | copy-start | bytes 3195076
  59.0 4.5 %copy-start.14 = (f32[516,516]{1,0:T(8,128)S(1)}, f32[516,516]{1,0:T(8,128)}, u32[]{:S(2)}) copy-start(f32[516,516]{1,0:T(8,128)} %copy-done.13) | copy-start | bytes 3195076
  65.8 2.2 %copy-start.25 = (bf16[516,512]{1,0:T(8,128)(2,1)S(1)}, bf16[516,512]{1,0:T(8,128)(2,1)}, u32[]{:S(2)}) copy-start(bf16[516,512]{1,0:T(8,128)(2,1)} %copy-done.23) | copy-start | bytes 1585156
  74.2 2.2 %copy-start.27 = (bf16[516,512]{1,0:T(8,128)(2,1)S(1)}, bf16[516,512]{1,0:T(8,128)(2,1)}, u32[]{:S(2)}) copy-start(bf16[516,512]{1,0:T(8,128)(2,1)} %copy-done.23) | copy-start | bytes 1585156
  93.5 53.8 %reduce-scatter.5.cloned.1.call-start = ((), (), s32[]{:S(2)}) async-start(), calls=%async_computation.4 | async-start | bytes 2408448 | tf_op jit(solution)/shard_map/reduce_scatter | solution.py:137
  107.7 8.6 %collective-permute-start.2 = (bf16[2,1,128,512]{3,2,0,1:T(8,128)(2,1)S(1)}, bf16[2,1,128,512]{3,2,0,1:T(8,128)(2,1)S(1)}, u32[]{:S(2)}, u32[]{:S(2)}) collective-permute-start(bf16[2,1,128,512]{3,2,0,1:T(8,128)(2,1)S(1)} %bitcast.71), channel_id=1, source_target_pairs={{0,2},{2,0},{4,6},{6,4},{8,10},{10,8},{12,14},{14,12},{16,18},{18,... | collective-permute-start | bytes 786440 | tf_op jit(solution)/shard_map/ppermute | solution.py:15
  116.4 7.8 %collective-permute-start.3 = (bf16[1,2,128,512]{3,2,1,0:T(8,128)(2,1)S(1)}, bf16[1,2,128,512]{3,2,1,0:T(8,128)(2,1)S(1)}, u32[]{:S(2)}, u32[]{:S(2)}) collective-permute-start(bf16[1,2,128,512]{3,2,1,0:T(8,128)(2,1)S(1)} %get-tuple-element.76), channel_id=1, source_target_pairs={{0,4},{2,6},{4,0},{6,2},{8,12},{10,14},{12,8},{14,10},{16,20},{18,... | collective-permute-start | bytes 786440 | tf_op jit(solution)/shard_map/ppermute | solution.py:15
  125.6 3.0 %copy-start.20 = (f32[1024]{0:T(1024)S(1)}, f32[1024]{0:T(1024)}, u32[]{:S(2)}) copy-start(f32[1024]{0:T(1024)} %param.19) | copy-start | bytes 12292
  (14 other events, 23.3 us)
Sparse Core Ops, SparseCore 0:
  31.2 10.2 all-gather.1
  93.7 10.8 reduce-scatter.2
  137.4 9.9 reduce-scatter.4
where the time goes:
time: 158 us; the launch traced here: 157 us
  waiting for transfers between devices  52.1 us (33%)
  matrix products  47.5 us (30%)
  other arithmetic  22 us (14%)
  between operations  14.6 us (9%)
  starting transfers between devices  9.06 us (6%)
  local copies, waits for them, and re-layouts  8.96 us (6%)
  blocking collectives  2.38 us (2%)
    dot_general x24, matrix products, attend(): return jnp.dot(weights, values, preferred_element_type=jnp.float32)  26.2 us
    ppermute x4, waiting for transfers between devices, partner(): lax.ppermute(x, axis, [(i, i ^ 1 << stride) for i in range(lax.axis_size(...  23.6 us
    reduce_scatter x1, waiting for transfers between devices, body(): lax.psum_scatter(projected, 'mp', scatter_dimension=1, tiled=True)  10.7 us
    reduce_scatter x1, waiting for transfers between devices, body(): added = lax.psum_scatter(partial_sum, 'mp', scatter_dimension=1, tiled=True)  10.1 us
    dot_general x1, matrix products, body(): partial_sum = jnp.dot(active, w_down, preferred_element_type=jnp.float32)  8.69 us
    ppermute x4, starting transfers between devices, partner(): lax.ppermute(x, axis, [(i, i ^ 1 << stride) for i in range(lax.axis_size(...  8.5 us
    all_gather x1, waiting for transfers between devices, body(): whole = lax.all_gather(rows, 'mp', axis=1, tiled=True)  7.67 us
    reduce_max x3, other arithmetic, attend(): top = jnp.max(masked, axis=-1, keepdims=True)  5.83 us
  transfers between devices with their start and end apart: 7, of which 7 were waited for; matrix products, arithmetic and copies ran while one was open for 2% of the time, Pallas kernels for 0%

commit v1 on v0

v1 whole, which is shorter than its diff:
```python
import functools

import jax
import jax.numpy as jnp
from jax import lax
from jax.experimental import pallas as pl
from jax.experimental.pallas import tpu as pltpu
from jax.sharding import PartitionSpec as P

HEAD_DIM = 64
GROUP = 4
EPS = 1e-05
NEG = -1e30
EXTRA = 16
BF16 = jnp.bfloat16
F32 = jnp.float32


def layer_norm(halves, gain):
    x = jnp.concatenate([h.astype(F32) for h in halves], axis=1)
    mean = jnp.mean(x, axis=-1, keepdims=True)
    centred = x - mean
    moment = jnp.mean(centred * centred, axis=-1, keepdims=True)
    return (centred * lax.rsqrt(moment + EPS) * gain).astype(BF16)


def dot(a, b):
    return jnp.dot(a, b, preferred_element_type=F32)


def kernel(
    blk,
    nb,
    video_ref,
    map_ref,
    tok_hbm,
    bot_ref,
    g1_ref,
    g2_ref,
    wqkv_hbm,
    wout_hbm,
    wup_hbm,
    wdown_hbm,
    out_ref,
    outb_ref,
    tok,
    wqkv,
    wout,
    wup,
    wdown,
    snd,
    x,
    ext,
    q,
    k,
    v,
    ctx,
    bias,
    ps1,
    pr1,
    own1,
    aft,
    act,
    ps2,
    pr2,
    own2,
    fin,
    ret,
    ld_sem,
    send_sem,
    recv_sem,
):
    slots = tok.shape[0]
    width = tok.shape[2]
    pairs = q.shape[0]
    keys = k.shape[1]
    rows = x.shape[1]
    ff = wup.shape[1]
    total = GROUP * blk

    me = lax.axis_index("clip")
    core = lax.axis_index("mp")
    peer = 1 - core
    bit0 = lax.rem(me, 2)
    bit1 = lax.rem(lax.div(me, 2), 2)
    flip0 = 1 - 2 * bit0
    flip1 = 2 - 4 * bit1
    partner = [me, me + flip0, me + flip1, me + flip0 + flip1]

    loads = [pltpu.make_async_copy(tok_hbm, tok, ld_sem.at[0])]
    loads.append(pltpu.make_async_copy(wqkv_hbm, wqkv, ld_sem.at[1]))
    for h in range(2):
        cols = pl.ds(h * width, width)
        loads.append(pltpu.make_async_copy(wout_hbm.at[:, cols], wout.at[h], ld_sem.at[2 + h]))
    loads.append(pltpu.make_async_copy(wup_hbm, wup, ld_sem.at[4]))
    for h in range(2):
        cols = pl.ds(h * width, width)
        loads.append(pltpu.make_async_copy(wdown_hbm.at[:, cols], wdown.at[h], ld_sem.at[5 + h]))
    for load in loads:
        load.start()

    barrier = pltpu.get_barrier_semaphore()
    for r in range(1, GROUP):
        pl.semaphore_signal(barrier, inc=1, device_id={"clip": partner[r]})
    pl.semaphore_signal(barrier, inc=1, device_id={"mp": peer})

    entry = [map_ref[me, s] for s in range(slots)]
    own = [jnp.where(e >= 0, lax.div(e, GROUP), -1) for e in entry]
    pick = []
    for r in range(GROUP):
        chosen = jnp.int32(0)
        for s in range(slots):
            chosen = jnp.where(own[s] == partner[r], s, chosen)
        pick.append(chosen)
    video = video_ref[me]
    mode = []
    for r in range(GROUP):
        m = jnp.int32(-1)
        for s in range(slots):
            e = map_ref[partner[r], s]
            mine = (e >= 0) & (lax.div(e, GROUP) == me)
            m = jnp.where(mine, jnp.where(lax.rem(e, GROUP) < video, 0, 1), m)
        mode.append(m)

    place = [(GROUP - 1) * blk] + [(r - 1) * blk for r in range(1, GROUP)]
    span = [pl.ds(place[0], blk + EXTRA)] + [pl.ds(place[r], blk) for r in range(1, GROUP)]
    size = [blk + EXTRA] + [blk] * (GROUP - 1)

    def ici(r, src, dst, base):
        return pltpu.make_async_remote_copy(
            src_ref=src,
            dst_ref=dst,
            send_sem=send_sem.at[base + r],
            recv_sem=recv_sem.at[base + r],
            device_id={"clip": partner[r]},
        )

    def d2d(r, src, dst, base):
        return pltpu.make_async_remote_copy(
            src_ref=src,
            dst_ref=dst,
            send_sem=send_sem.at[base + r],
            recv_sem=recv_sem.at[base + r],
            device_id={"mp": peer},
        )

    half = x.at[core]
    arrive = [ici(r, snd.at[r - 1], half.at[span[r]], 0) if r else None for r in range(GROUP)]
    share = [d2d(r, half.at[span[r]], half.at[span[r]], 4) for r in range(GROUP)]
    proj = [d2d(r, ps1.at[span[r]], pr1.at[span[r]], 8) for r in range(GROUP)]
    joined = [d2d(r, aft.at[core].at[span[r]], aft.at[core].at[span[r]], 12) for r in range(GROUP)]
    down = [d2d(r, ps2.at[span[r]], pr2.at[span[r]], 16) for r in range(GROUP)]
    back = [ici(r, fin.at[r - 1], ret.at[r], 20) if r else None for r in range(GROUP)]

    loads[0].wait()
    for r in range(1, GROUP):
        snd[r - 1] = tok[pick[r]]
    x[core, pl.ds(place[0], blk)] = tok[pick[0]]
    small = bot_ref[0].astype(F32)
    for i in range(EXTRA // nb):
        ext[pl.ds(i * nb, nb)] = small
    x[core, pl.ds(total, EXTRA)] = ext[...].astype(BF16)

    pl.semaphore_wait(barrier, GROUP)
    for r in (1, 2, 3):
        arrive[r].start()
    share[0].start()

    column = lax.broadcasted_iota(jnp.int32, (1, keys), 1)
    extra_key = (column >= total) & (column < total + nb)
    key_mode = jnp.full((1, keys), -1, jnp.int32)
    for r in range(GROUP):
        inside = (column >= place[r]) & (column < place[r] + blk)
        key_mode = jnp.where(inside, mode[r], key_mode)

    def bias_of(m):
        return jnp.where(extra_key | ((key_mode == m) & (key_mode >= 0)), 0.0, NEG).astype(F32)

    row_bias = [bias_of(mode[r]) for r in range(GROUP)]
    bias[pl.ds(0, blk)] = jnp.broadcast_to(row_bias[0], (blk, keys))
    line = lax.broadcasted_iota(jnp.int32, (EXTRA, keys), 0)
    bias[pl.ds(blk, EXTRA)] = jnp.where(
        (line >= nb) & (line < 2 * nb),
        jnp.broadcast_to(bias_of(1), (EXTRA, keys)),
        jnp.broadcast_to(bias_of(0), (EXTRA, keys)),
    )
    for j in range(pairs):
        k[j, pl.ds(rows, keys - rows)] = jnp.zeros((keys - rows, 128), BF16)
        v[j, pl.ds(rows, keys - rows)] = jnp.zeros((keys - rows, 128), BF16)

    def project(r):
        n = layer_norm([x[0, span[r]], x[1, span[r]]], g1_ref[...])
        for i, target in enumerate((q, k, v)):
            y = dot(n, wqkv[i])
            if i == 0:
                y = y.astype(BF16).astype(F32) * HEAD_DIM ** (-0.5)
            y = y.astype(BF16)
            for j in range(pairs):
                target[j, span[r]] = y[:, j * 128 : (j + 1) * 128]

    loads[1].wait()
    share[0].wait_recv()
    project(0)
    for r in (1, 2):
        arrive[r].wait_recv()
        share[r].start()
    for r in (1, 2):
        share[r].wait_recv()
        project(r)
    arrive[3].wait_recv()
    share[3].start()
    share[3].wait_recv()
    project(3)

    def attend(r):
        lane = lax.broadcasted_iota(jnp.int32, (1, 128), 1)

        def step(j, _):
            qs = q[j, span[r]]
            ks = k[j]
            vs = v[j]
            outs = []
            for h in range(2):
                sel = (lane < HEAD_DIM) if h == 0 else (lane >= HEAD_DIM)
                qh = jnp.where(sel, qs, jnp.zeros_like(qs))
                s = lax.dot_general(qh, ks, (((1,), (1,)), ((), ())), preferred_element_type=F32)
                s = s + (bias[...] if r == 0 else row_bias[r])
                top = jnp.max(s, axis=-1, keepdims=True)
                p = jnp.exp(s - top)
                norm = jnp.sum(p, axis=-1, keepdims=True)
                outs.append(dot(p.astype(BF16), vs) / norm)
            o = jnp.where(lane < HEAD_DIM, outs[0], outs[1])
            if r == 0:
                ctx[j, pl.ds(place[0], blk)] = o[:blk].astype(BF16)
                e = o[blk:]
                e = 0.5 * (e + pltpu.roll(e, EXTRA - nb, 0))
                ctx[j, pl.ds(total, EXTRA)] = e.astype(BF16)
            else:
                ctx[j, span[r]] = o.astype(BF16)
            return 0

        lax.fori_loop(0, pairs, step, 0)

    def stage_a(r):
        attend(r)
        c = jnp.concatenate([ctx[j, span[r]] for j in range(pairs)], axis=1)
        ps1[span[r]] = dot(c, wout[peer]).astype(BF16)
        proj[r].start()
        own1[span[r]] = dot(c, wout[core])

    def stage_b(r):
        proj[r].wait_recv()
        total_sum = x[core, span[r]].astype(F32) + (own1[span[r]] + pr1[span[r]].astype(F32))
        aft[core, span[r]] = total_sum.astype(BF16)
        joined[r].start()

    def stage_c(r):
        joined[r].wait_recv()
        n = layer_norm([aft[0, span[r]], aft[1, span[r]]], g2_ref[...])
        tile = width
        for t in range(ff // tile):
            up = dot(n, wup[:, t * tile : (t + 1) * tile])
            act[pl.ds(0, size[r]), t * tile : (t + 1) * tile] = jax.nn.gelu(up, approximate=True).astype(BF16)
        a = act[pl.ds(0, size[r])]
        ps2[span[r]] = dot(a, wdown[peer]).astype(BF16)
        down[r].start()
        own2[span[r]] = dot(a, wdown[core])

    def stage_d(r):
        down[r].wait_recv()
        merged = aft[core, span[r]].astype(F32) + (own2[span[r]] + pr2[span[r]].astype(F32))
        if r == 0:
            ret[0] = merged[:blk].astype(BF16)
            outb_ref[0] = merged[blk : blk + nb].astype(BF16)
        else:
            fin[r - 1] = merged.astype(BF16)
            back[r].start()

    loads[2].wait()
    loads[3].wait()
    stage_a(3)
    stage_a(1)
    stage_b(3)
    stage_a(2)
    stage_b(1)
    for load in loads[4:]:
        load.wait()
    stage_c(3)
    stage_a(0)
    stage_b(2)
    stage_d(3)
    stage_c(1)
    stage_b(0)
    stage_d(1)
    stage_c(2)
    stage_d(2)
    stage_c(0)
    stage_d(0)
    for r in (3, 1, 2):
        back[r].wait_recv()
    for s in range(slots):
        where = jnp.int32(0)
        for r in range(GROUP):
            where = jnp.where(own[s] == partner[r], r, where)
        live = jnp.where(entry[s] >= 0, 1.0, 0.0).astype(F32)
        block = ret[where].astype(F32)
        out_ref[s] = (block * live).astype(BF16)
    for r in range(1, GROUP):
        arrive[r].wait_send()
        back[r].wait_send()
    for r in range(GROUP):
        for c in (share, proj, joined, down):
            c[r].wait_send()


def body(
    tokens,
    bottleneck,
    clip_lengths,
    video_blocks,
    store_map,
    norm1_gain,
    w_qkv,
    w_out,
    norm2_gain,
    w_up,
    w_down,
):
    slots, blk, width = tokens.shape
    nb = bottleneck.shape[1]
    dim = w_qkv.shape[1]
    inner = w_qkv.shape[2]
    ff = w_up.shape[1]
    pairs = inner // 128
    rows = GROUP * blk + EXTRA
    keys = (rows + 127) // 128 * 128
    smem = pl.BlockSpec(memory_space=pltpu.SMEM)
    vmem = pl.BlockSpec(memory_space=pltpu.VMEM)
    hbm = pl.BlockSpec(memory_space=pl.ANY)
    V = pltpu.VMEM
    return pl.pallas_call(
        functools.partial(kernel, blk, nb),
        out_shape=(
            jax.ShapeDtypeStruct(tokens.shape, BF16),
            jax.ShapeDtypeStruct(bottleneck.shape, BF16),
        ),
        in_specs=[smem, smem, hbm, vmem, vmem, vmem, hbm, hbm, hbm, hbm],
        out_specs=(vmem, vmem),
        scratch_shapes=[
            V((slots, blk, width), BF16),
            V(w_qkv.shape, BF16),
            V((2, inner, width), BF16),
            V(w_up.shape, BF16),
            V((2, ff, width), BF16),
            V((GROUP - 1, blk, width), BF16),
            V((2, rows, width), BF16),
            V((EXTRA, width), F32),
            V((pairs, rows, 128), BF16),
            V((pairs, keys, 128), BF16),
            V((pairs, keys, 128), BF16),
            V((pairs, rows, 128), BF16),
            V((blk + EXTRA, keys), F32),
            V((rows, width), BF16),
            V((rows, width), BF16),
            V((rows, width), F32),
            V((2, rows, width), BF16),
            V((blk + EXTRA, ff), BF16),
            V((rows, width), BF16),
            V((rows, width), BF16),
            V((rows, width), F32),
            V((GROUP - 1, blk, width), BF16),
            V((GROUP, blk, width), BF16),
            pltpu.SemaphoreType.DMA((7,)),
            pltpu.SemaphoreType.DMA((24,)),
            pltpu.SemaphoreType.DMA((24,)),
        ],
        compiler_params=pltpu.CompilerParams(collective_id=0, has_side_effects=True),
        name="merge_layer",
    )(
        video_blocks,
        store_map,
        tokens,
        bottleneck,
        norm1_gain.reshape(1, dim),
        norm2_gain.reshape(1, dim),
        w_qkv,
        w_out,
        w_up,
        w_down,
    )


def solution(mesh):
    placed = (
        P("clip", None, "mp"),
        P("clip", None, "mp"),
        P(),
        P(),
        P(),
        P(),
        P(None, None, "mp"),
        P("mp", None),
        P(),
        P(None, "mp"),
        P("mp", None),
    )
    return jax.shard_map(
        body,
        mesh=mesh,
        in_specs=placed,
        out_specs=(P("clip", None, "mp"), P("clip", None, "mp")),
        check_vma=False,
    )
```

time: 158 us -> 46.5 us (0.29)
  waiting for transfers between devices: 52.1 us -> 0 us
  matrix products: 47.5 us -> 0 us
  Pallas kernels: 0 us -> 41.2 us
  other arithmetic: 22 us -> 0 us
  between operations: 14.6 us -> 0.64 us
  starting transfers between devices: 9.06 us -> 0 us
  local copies, waits for them, and re-layouts: 8.96 us -> 4.39 us
  blocking collectives: 2.38 us -> 0 us
    dot_general x41 -> x0, matrix products: 47.5 us -> none  [the longest x24 26.2 us: attend(): return jnp.dot(weights, values, preferred_element_type=jnp.float32)]
    pallas_call x0 -> x1, Pallas kernels: none -> 41.2 us  [body(): pl.pallas_call(functools.partial(kernel, blk, nb), out_shape=(jax.ShapeDt...]
    ppermute x4 -> x0, waiting for transfers between devices: 23.6 us -> none  [partner(): lax.ppermute(x, axis, [(i, i ^ 1 << stride) for i in range(lax.axis_size(...]
    reduce_scatter x2 -> x0, waiting for transfers between devices: 20.8 us -> none  [the longest x1 10.7 us: body(): lax.psum_scatter(projected, 'mp', scatter_dimension=1, tiled=True)]
    ppermute x4 -> x0, starting transfers between devices: 8.5 us -> none  [partner(): lax.ppermute(x, axis, [(i, i ^ 1 << stride) for i in range(lax.axis_size(...]
    reduce_sum x7 -> x0, other arithmetic: 8.06 us -> none  [the longest x3 5.52 us: attend(): jnp.sum(weights, axis=-1, keepdims=True)]
    all_gather x1 -> x0, waiting for transfers between devices: 7.67 us -> none  [body(): whole = lax.all_gather(rows, 'mp', axis=1, tiled=True)]
    reduce_max x3 -> x0, other arithmetic: 5.83 us -> none  [attend(): top = jnp.max(masked, axis=-1, keepdims=True)]
  transfers between devices with their start and end apart: 7 -> 0, of which waited for: 7 -> 0; matrix products, arithmetic and copies ran while one was open for 2% -> 0% of each run, Pallas kernels for 0% -> 0%
where the time goes in v1:
time: 46.5 us; the launch traced here: 46.2 us
  Pallas kernels  41.2 us (89%)
  local copies, waits for them, and re-layouts  4.39 us (9%)
  between operations  0.64 us (1%)
    pallas_call x1, Pallas kernels, body(): pl.pallas_call(functools.partial(kernel, blk, nb), out_shape=(jax.ShapeDt...  41.2 us
    unnamed x3, local copies, waits for them, and re-layouts  4.39 us

profile of v1, /device:TPU:0, one launch (start us, length us, event | category | flops | bytes accessed | tf_op | source)
XLA Modules:
  0.0 46.2 jit_solution(18197536557256272203)
XLA Ops:
  0.6 1.4 %copy.12.map_ref = s32[16,3]{1,0:T(8,128)} copy(s32[16,3]{0,1:T(4,128)} %param.14) | data formatting | bytes 384 | tf_op args[4]
  2.0 41.2 %merge_layer.1 = (bf16[3,128,512]{2,1,0:T(8,128)(2,1)}, bf16[1,4,512]{2,1,0:T(4,128)(2,1)}) custom-call(s32[16]{0:T(128)} %video_ref.1, s32[16,3]{1,0:T(8,128)} %copy.12.map_ref, bf16[3,128,512]{2,1,0:T(8,128)(2,1)} %tok_hbm.1, bf16[1,4,512]{2,1,0:T(4,128)(2,1)} %bot_ref.1, f32[1,1024]{1,0:T(1,128)} %bitcast.2, f32[1,1024]{1,0:T(1,128)} %bitcast.3, ...), custom_call_target="tpu_custom_call" | custom-call | tf_op jit(solution)/shard_map/merge_layer/pallas_call | solution.py:341
  43.2 1.8 %copy.15 = bf16[3,128,512]{2,1,0:T(8,128)(2,1)} copy(bf16[3,128,512]{2,1,0:T(8,128)(2,1)} %get-tuple-element.4) | data formatting | bytes 786432
  45.0 1.3 %copy.16 = bf16[1,4,512]{2,1,0:T(4,128)(2,1)} copy(bf16[1,4,512]{2,1,0:T(4,128)(2,1)} %get-tuple-element.5) | data formatting | bytes 8192

commit v2 on v1

--- a/solution.py
+++ b/solution.py
@@ -12,6 +12,7 @@
 EPS = 1e-05
 NEG = -1e30
 EXTRA = 16
+UNROLL = True
 BF16 = jnp.bfloat16
 F32 = jnp.float32
 
@@ -104,7 +105,7 @@
         pl.semaphore_signal(barrier, inc=1, device_id={"clip": partner[r]})
     pl.semaphore_signal(barrier, inc=1, device_id={"mp": peer})
 
-    entry = [map_ref[me, s] for s in range(slots)]
+    entry = [map_ref[s, me] for s in range(slots)]
     own = [jnp.where(e >= 0, lax.div(e, GROUP), -1) for e in entry]
     pick = []
     for r in range(GROUP):
@@ -117,7 +118,7 @@
     for r in range(GROUP):
         m = jnp.int32(-1)
         for s in range(slots):
-            e = map_ref[partner[r], s]
+            e = map_ref[s, partner[r]]
             mine = (e >= 0) & (lax.div(e, GROUP) == me)
             m = jnp.where(mine, jnp.where(lax.rem(e, GROUP) < video, 0, 1), m)
         mode.append(m)
@@ -186,7 +187,8 @@
     )
     for j in range(pairs):
         k[j, pl.ds(rows, keys - rows)] = jnp.zeros((keys - rows, 128), BF16)
-        v[j, pl.ds(rows, keys - rows)] = jnp.zeros((keys - rows, 128), BF16)
+        v[j, pl.ds(rows, keys - rows), :128] = jnp.zeros((keys - rows, 128), BF16)
+        v[j, :, 128:] = jnp.ones((keys, 128), BF16)
 
     def project(r):
         n = layer_norm([x[0, span[r]], x[1, span[r]]], g1_ref[...])
@@ -196,7 +198,7 @@
                 y = y.astype(BF16).astype(F32) * HEAD_DIM ** (-0.5)
             y = y.astype(BF16)
             for j in range(pairs):
-                target[j, span[r]] = y[:, j * 128 : (j + 1) * 128]
+                target[j, span[r], :128] = y[:, j * 128 : (j + 1) * 128]
 
     loads[1].wait()
     share[0].wait_recv()
@@ -214,22 +216,25 @@
 
     def attend(r):
         lane = lax.broadcasted_iota(jnp.int32, (1, 128), 1)
+        low = lane < HEAD_DIM
 
         def step(j, _):
             qs = q[j, span[r]]
-            ks = k[j]
-            vs = v[j]
-            outs = []
-            for h in range(2):
-                sel = (lane < HEAD_DIM) if h == 0 else (lane >= HEAD_DIM)
-                qh = jnp.where(sel, qs, jnp.zeros_like(qs))
-                s = lax.dot_general(qh, ks, (((1,), (1,)), ((), ())), preferred_element_type=F32)
-                s = s + (bias[...] if r == 0 else row_bias[r])
-                top = jnp.max(s, axis=-1, keepdims=True)
-                p = jnp.exp(s - top)
-                norm = jnp.sum(p, axis=-1, keepdims=True)
-                outs.append(dot(p.astype(BF16), vs) / norm)
-            o = jnp.where(lane < HEAD_DIM, outs[0], outs[1])
+            zero = jnp.zeros_like(qs)
+            both = jnp.concatenate([jnp.where(low, qs, zero), jnp.where(low, zero, qs)], axis=0)
+            s = lax.dot_general(both, k[j], (((1,), (1,)), ((), ())), preferred_element_type=F32)
+            if r == 0:
+                b = bias[...]
+                s = s + jnp.concatenate([b, b], axis=0)
+            else:
+                s = s + row_bias[r]
+            top = jnp.max(s, axis=-1, keepdims=True)
+            p = jnp.exp(s - top).astype(BF16)
+            o = dot(p, v[j])
+            m = size[r]
+            over = jnp.where(low, o[:m, :128], o[m:, :128])
+            under = jnp.where(low, o[:m, 128:], o[m:, 128:])
+            o = over / under
             if r == 0:
                 ctx[j, pl.ds(place[0], blk)] = o[:blk].astype(BF16)
                 e = o[blk:]
@@ -239,7 +244,7 @@
                 ctx[j, span[r]] = o.astype(BF16)
             return 0
 
-        lax.fori_loop(0, pairs, step, 0)
+        lax.fori_loop(0, pairs, step, 0, unroll=UNROLL)
 
     def stage_a(r):
         attend(r)
@@ -357,7 +362,7 @@
             V((EXTRA, width), F32),
             V((pairs, rows, 128), BF16),
             V((pairs, keys, 128), BF16),
-            V((pairs, keys, 128), BF16),
+            V((pairs, keys, 256), BF16),
             V((pairs, rows, 128), BF16),
             V((blk + EXTRA, keys), F32),
             V((rows, width), BF16),
@@ -378,7 +383,7 @@
         name="merge_layer",
     )(
         video_blocks,
-        store_map,
+        store_map.T,
         tokens,
         bottleneck,
         norm1_gain.reshape(1, dim),

time: 46.5 us -> 38.3 us (0.82)
  Pallas kernels: 41.2 us -> 34.4 us
  local copies, waits for them, and re-layouts: 4.39 us -> 3.03 us
    pallas_call x1, Pallas kernels: 41.2 us -> 34.4 us  [body(): pl.pallas_call(functools.partial(kernel, blk, nb), out_shape=(jax.ShapeDt...]
    unnamed x3 -> x2, local copies, waits for them, and re-layouts: 4.39 us -> 3.03 us
where the time goes in v2:
time: 38.3 us; the launch traced here: 38.1 us
  Pallas kernels  34.4 us (90%)
  local copies, waits for them, and re-layouts  3.03 us (8%)
  between operations  0.64 us (2%)
    pallas_call x1, Pallas kernels, body(): pl.pallas_call(functools.partial(kernel, blk, nb), out_shape=(jax.ShapeDt...  34.4 us
    unnamed x2, local copies, waits for them, and re-layouts  3.03 us

profile of v2, /device:TPU:0, one launch (start us, length us, event | category | flops | bytes accessed | tf_op | source)
XLA Modules:
  0.0 38.1 jit_solution(10372636090722246504)
XLA Ops:
  0.6 34.4 %merge_layer.1 = (bf16[3,128,512]{2,1,0:T(8,128)(2,1)}, bf16[1,4,512]{2,1,0:T(4,128)(2,1)}) custom-call(s32[16]{0:T(128)} %video_ref.1, s32[3,16]{1,0:T(4,128)} %bitcast.5, bf16[3,128,512]{2,1,0:T(8,128)(2,1)} %tok_hbm.1, bf16[1,4,512]{2,1,0:T(4,128)(2,1)} %bot_ref.1, f32[1,1024]{1,0:T(1,128)} %bitcast.3, f32[1,1024]{1,0:T(1,128)} %bitcast.4, ...), custom_call_target="tpu_custom_call" | custom-call | tf_op jit(solution)/shard_map/merge_layer/pallas_call | solution.py:346
  35.1 1.8 %copy.14 = bf16[3,128,512]{2,1,0:T(8,128)(2,1)} copy(bf16[3,128,512]{2,1,0:T(8,128)(2,1)} %get-tuple-element.4) | data formatting | bytes 786432
  36.8 1.3 %copy.15 = bf16[1,4,512]{2,1,0:T(4,128)(2,1)} copy(bf16[1,4,512]{2,1,0:T(4,128)(2,1)} %get-tuple-element.5) | data formatting | bytes 8192

commit v3 on v2

--- a/solution.py
+++ b/solution.py
@@ -97,8 +97,7 @@
     for h in range(2):
         cols = pl.ds(h * width, width)
         loads.append(pltpu.make_async_copy(wdown_hbm.at[:, cols], wdown.at[h], ld_sem.at[5 + h]))
-    for load in loads:
-        load.start()
+    loads[0].start()
 
     barrier = pltpu.get_barrier_semaphore()
     for r in range(1, GROUP):
@@ -166,6 +165,8 @@
     for r in (1, 2, 3):
         arrive[r].start()
     share[0].start()
+    for load in loads[1:]:
+        load.start()
 
     column = lax.broadcasted_iota(jnp.int32, (1, keys), 1)
     extra_key = (column >= total) & (column < total + nb)
@@ -318,6 +319,11 @@
             c[r].wait_send()
 
 
+def place(stored_ref, merged_ref, out_ref, outb_ref):
+    out_ref[...] = stored_ref[...]
+    outb_ref[...] = merged_ref[...]
+
+
 def body(
     tokens,
     bottleneck,
@@ -343,7 +349,7 @@
     vmem = pl.BlockSpec(memory_space=pltpu.VMEM)
     hbm = pl.BlockSpec(memory_space=pl.ANY)
     V = pltpu.VMEM
-    return pl.pallas_call(
+    stored, merged = pl.pallas_call(
         functools.partial(kernel, blk, nb),
         out_shape=(
             jax.ShapeDtypeStruct(tokens.shape, BF16),
@@ -393,6 +399,16 @@
         w_up,
         w_down,
     )
+    return pl.pallas_call(
+        place,
+        out_shape=(
+            jax.ShapeDtypeStruct(tokens.shape, BF16),
+            jax.ShapeDtypeStruct(bottleneck.shape, BF16),
+        ),
+        in_specs=[vmem, vmem],
+        out_specs=(vmem, vmem),
+        name="place",
+    )(stored, merged)
 
 
 def solution(mesh):

time: 38.3 us -> 37.1 us (0.969)
  local copies, waits for them, and re-layouts: 3.03 us -> 0 us
  Pallas kernels: 34.4 us -> 36.2 us
    unnamed x2 -> x0, local copies, waits for them, and re-layouts: 3.03 us -> none
    pallas_call x0 -> x1, Pallas kernels: none -> 1.77 us  [body(): pl.pallas_call(place, out_shape=(jax.ShapeDtypeStruct(tokens.shape, BF16)...]
where the time goes in v3:
time: 37.1 us; the launch traced here: 36.8 us
  Pallas kernels  36.2 us (98%)
  between operations  0.64 us (2%)
    pallas_call x1, Pallas kernels, body(): pl.pallas_call(functools.partial(kernel, blk, nb), out_shape=(jax.ShapeDt...  34.4 us
    pallas_call x1, Pallas kernels, body(): pl.pallas_call(place, out_shape=(jax.ShapeDtypeStruct(tokens.shape, BF16)...  1.77 us

profile of v3, /device:TPU:0, one launch (start us, length us, event | category | flops | bytes accessed | tf_op | source)
XLA Modules:
  0.0 36.8 jit_solution(16674849684625015356)
XLA Ops:
  0.6 34.4 %merge_layer.1 = (bf16[3,128,512]{2,1,0:T(8,128)(2,1)}, bf16[1,4,512]{2,1,0:T(4,128)(2,1)}) custom-call(s32[16]{0:T(128)} %video_ref.1, s32[3,16]{1,0:T(4,128)} %bitcast.5, bf16[3,128,512]{2,1,0:T(8,128)(2,1)} %tok_hbm.1, bf16[1,4,512]{2,1,0:T(4,128)(2,1)} %bot_ref.1, f32[1,1024]{1,0:T(1,128)} %bitcast.3, f32[1,1024]{1,0:T(1,128)} %bitcast.4, ...), custom_call_target="tpu_custom_call" | custom-call | tf_op jit(solution)/shard_map/merge_layer/pallas_call | solution.py:352
  35.1 1.8 %place.1 = (bf16[3,128,512]{2,1,0:T(8,128)(2,1)}, bf16[1,4,512]{2,1,0:T(4,128)(2,1)}) custom-call(bf16[3,128,512]{2,1,0:T(8,128)(2,1)} %get-tuple-element.4.stored_ref, bf16[1,4,512]{2,1,0:T(4,128)(2,1)} %get-tuple-element.5.merged_ref), custom_call_target="tpu_custom_call" | custom-call | tf_op jit(solution)/shard_map/place/pallas_call | solution.py:402
